TPU v7x, 32 devices: a whole 2x2x4 slice. The times are simulated.
32 devices in a mesh: dp: 2 (over x), tp: 16 (over y, z, core).
Axes of the slice: x: 2, y: 2, z: 4, core: 2. Of those that a mesh axis runs over, the one named last changes fastest.
Arguments:
- x: bfloat16 [4096, 2048], P('dp'), parts along dimension 0
- dy: bfloat16 [4096, 2048], P('dp'), parts along dimension 0
- gate: bfloat16 [4096, 8192], P('dp', 'tp'), parts along dimension 0
- up: bfloat16 [4096, 8192], P('dp', 'tp'), parts along dimension 0
- w_gate: bfloat16 [2048, 8192], P(None, 'tp')
- w_up: bfloat16 [2048, 8192], P(None, 'tp')
- w_down: bfloat16 [8192, 2048], P('tp')
Outputs:
- output 1: bfloat16 [4096, 2048], P('dp'), parts along dimension 0
- output 2: bfloat16 [4096, 8192], P('dp', 'tp'), parts along dimension 0
- output 3: bfloat16 [4096, 8192], P('dp', 'tp'), parts along dimension 0
- output 4: bfloat16 [16384, 2048], P(('dp', 'tp')), parts along dimension 0
There are 2 independent parts. A program takes and returns all parts, laid end to end along the dimension named above; an argument that names none is the same for every part.
All inputs are finite; a program needn't handle non-finite values.
Results may differ from a plain program's by a relative error of at most 0.012.
Values are sent between devices in bfloat16 or wider.
A program may use at most 2 GiB of HBM per device.

v0:
```python
import jax
import jax.numpy as jnp
from jax import lax
from jax.sharding import PartitionSpec as P


def act(gate, up):
    return jax.nn.silu(gate) * up


def solution(mesh):
    def step(x, dy, gate, up, w_gate, w_up, w_down):
        hidden, back = jax.vjp(act, gate.astype(jnp.float32), up.astype(jnp.float32))
        d_hidden = jnp.dot(dy, w_down.T, preferred_element_type=jnp.float32)
        d_gate, d_up = (g.astype(jnp.bfloat16) for g in back(d_hidden))
        term = jnp.dot(d_gate, w_gate.T, preferred_element_type=jnp.float32) + jnp.dot(d_up, w_up.T, preferred_element_type=jnp.float32)
        dx = lax.psum(term.astype(jnp.bfloat16), "tp")
        dw_gate = jnp.dot(x.T, d_gate, preferred_element_type=jnp.float32)
        dw_up = jnp.dot(x.T, d_up, preferred_element_type=jnp.float32)
        dw_down = jnp.dot(hidden.astype(jnp.bfloat16).T, dy, preferred_element_type=jnp.float32)
        return dx, *(g.astype(jnp.bfloat16) for g in (dw_gate, dw_up, dw_down))

    tokens, columns, rows = P("dp", None), P(None, "tp"), P("tp", None)
    return jax.shard_map(
        step,
        mesh=mesh,
        in_specs=(tokens, tokens, P("dp", "tp"), P("dp", "tp"), columns, columns, rows),
        out_specs=(tokens, P("dp", "tp"), P("dp", "tp"), P(("dp", "tp"), None)),
        check_vma=False,
    )
```

profile of v0, /device:TPU:0, one launch (start us, length us, event | category | flops | bytes accessed | tf_op | source)
XLA Modules:
  0.0 233.5 jit_solution(7520645292408562636)
XLA Ops:
  7.2 0.0 copy-start
  7.2 0.0 all-reduce.2.cloned.1.call-start
  7.2 13.3 %fusion.6 = (bf16[2048,512]{1,0:T(8,128)(2,1)S(1)}, f32[2048,512]{1,0:T(8,128)}) fusion(bf16[2048,512]{1,0:T(8,128)(2,1)} %param.9, bf16[2048,512]{1,0:T(8,128)(2,1)} %param.10, bf16[2048,2048]{1,0:T(8,128)(2,1)} %param.8, bf16[512,2048]{1,0:T(8,128)(2,1)} %param.13), kind=kOutput, calls=%fused_computation.13 | convolution fusion | flops 4308598784 | bytes 20971520 | tf_op jit(solution)/shard_map/dot_general | solution.py:14
  20.6 0.0 copy-start.2
  20.6 0.0 copy-done
  20.6 8.3 %fusion.11 = f32[2048,2048]{1,0:T(8,128)} fusion(bf16[2048,512]{1,0:T(8,128)(2,1)S(1)} %get-tuple-element.8, bf16[2048,512]{1,0:T(8,128)(2,1)S(1)} %copy-done), kind=kOutput, calls=%fused_computation.21 | convolution fusion | flops 4294967296 | bytes 20971520 | tf_op jit(solution)/shard_map/dot_general | solution.py:16
  28.9 0.0 copy-done.2
  28.9 16.5 %add_convert_fusion = bf16[2048,2048]{1,0:T(8,128)(2,1)} fusion(f32[2048,2048]{1,0:T(8,128)} %fusion.11, bf16[2048,512]{1,0:T(8,128)(2,1)} %param.12, f32[2048,512]{1,0:T(8,128)} %get-tuple-element.9, bf16[2048,512]{1,0:T(8,128)(2,1)} %param.9), kind=kOutput, calls=%fused_computation | convolution fusion | flops 4310695936 | bytes 33554432 | tf_op jit(solution)/shard_map/dot_general | solution.py:16
  45.4 0.0 all-reduce.2.cloned.1.call-update
  45.4 8.6 %fusion.7 = bf16[2048,512]{0,1:T(8,128)(2,1)S(1)} fusion(bf16[2048,512]{1,0:T(8,128)(2,1)} %copy-done.2, bf16[2048,2048]{1,0:T(8,128)(2,1)} %param.7), kind=kOutput, calls=%fused_computation.18 | convolution fusion | flops 4296015872 | bytes 12582912 | tf_op jit(solution)/shard_map/dot_general | solution.py:18
  54.0 2.5 %copy.11 = bf16[2048,512]{1,0:T(8,128)(2,1)} copy(bf16[2048,512]{0,1:T(8,128)(2,1)S(1)} %fusion.7) | data formatting | bytes 4194304
  56.5 10.1 %fusion.8 = bf16[2048,512]{0,1:T(8,128)(2,1)S(1)} fusion(bf16[2048,2048]{1,0:T(8,128)(2,1)} %param.7, f32[2048,512]{1,0:T(8,128)} %get-tuple-element.9, bf16[2048,512]{1,0:T(8,128)(2,1)} %param.9), kind=kOutput, calls=%fused_computation.19 | convolution fusion | flops 4303355904 | bytes 16777216 | tf_op jit(solution)/shard_map/dot_general | solution.py:19
  66.7 2.5 %copy.12 = bf16[2048,512]{1,0:T(8,128)(2,1)} copy(bf16[2048,512]{0,1:T(8,128)(2,1)S(1)} %fusion.8) | data formatting | bytes 4194304
  69.2 11.1 %convolution_convert_fusion = bf16[512,2048]{1,0:T(8,128)(2,1)} fusion(bf16[2048,2048]{1,0:T(8,128)(2,1)} %param.8, bf16[2048,512]{1,0:T(8,128)(2,1)} %param.10, bf16[2048,512]{1,0:T(8,128)(2,1)} %param.9), kind=kOutput, calls=%fused_computation.15 | convolution fusion | flops 4304404480 | bytes 14680064 | tf_op jit(solution)/shard_map/dot_general | solution.py:20
  80.2 137.8 %all-reduce.2.cloned.1.call-done = bf16[2048,2048]{1,0:T(8,128)(2,1)} async-done(((bf16[2048,2048]{1,0:T(8,128)(2,1)}), bf16[2048,2048]{1,0:T(8,128)(2,1)}) %all-reduce.2.cloned.1.call-update) | async-done | bytes 8388624 | tf_op jit(solution)/shard_map/psum | solution.py:17
  218.1 0.0 copy-start.1
  218.1 8.6 %copy.14 = bf16[2048,2048]{1,0:T(8,128)(2,1)} copy(bf16[2048,2048]{1,0:T(8,128)(2,1)} %all-reduce.2.cloned.1.call-done) | data formatting | bytes 16777216
  226.7 0.0 copy-done.1
Async XLA Ops:
  7.2 13.4 %copy-start = (bf16[2048,512]{1,0:T(8,128)(2,1)S(1)}, bf16[2048,512]{1,0:T(8,128)(2,1)}, u32[]{:S(2)}) copy-start(bf16[2048,512]{1,0:T(8,128)(2,1)} %param.11) | copy-start | bytes 6291460
  7.2 210.9 %all-reduce.2.cloned.1.call-start = ((), (), s32[]{:S(2)}) async-start(), calls=%async_computation | async-start | bytes 16777216 | tf_op jit(solution)/shard_map/psum | solution.py:17
  20.6 8.3 %copy-start.2 = (bf16[2048,512]{1,0:T(8,128)(2,1)}, bf16[2048,512]{1,0:T(8,128)(2,1)S(1)}, u32[]{:S(2)}) copy-start(bf16[2048,512]{1,0:T(8,128)(2,1)S(1)} %get-tuple-element.8) | copy-start | bytes 6291460
  218.1 8.6 %copy-start.1 = (bf16[2048,512]{1,0:T(8,128)(2,1)S(1)}, bf16[2048,512]{1,0:T(8,128)(2,1)}, u32[]{:S(2)}) copy-start(bf16[2048,512]{1,0:T(8,128)(2,1)} %param.11) | copy-start | bytes 6291460
Sparse Core Ops, SparseCore 0:
  45.5 172.4 all-reduce.1
where the time goes:
time: 234 us
  waiting for transfers between devices  138 us (59%)
  matrix products  68 us (29%)
  between operations  14.1 us (6%)
  local copies, waits for them, and re-layouts  13.6 us (6%)
    psum x1, waiting for transfers between devices, step(): dx = lax.psum(term.astype(jnp.bfloat16), 'tp')  138 us
    dot_general x1, matrix products, step(): jnp.dot(d_up, w_up.T, preferred_element_type=jnp.float32)  16.5 us
    unnamed x9, local copies, waits for them, and re-layouts  13.6 us
    dot_general x1, matrix products, step(): d_hidden = jnp.dot(dy, w_down.T, preferred_element_type=jnp.float32)  13.3 us
    dot_general x1, matrix products, step(): jnp.dot(hidden.astype(jnp.bfloat16).T, dy, preferred_element_type=jnp.flo...  11.1 us
    dot_general x1, matrix products, step(): dw_up = jnp.dot(x.T, d_up, preferred_element_type=jnp.float32)  10.1 us
    dot_general x1, matrix products, step(): dw_gate = jnp.dot(x.T, d_gate, preferred_element_type=jnp.float32)  8.59 us
    dot_general x1, matrix products, step(): jnp.dot(d_gate, w_gate.T, preferred_element_type=jnp.float32)  8.33 us
  transfers between devices with their start and end apart: 1, of which 1 were waited for; matrix products, arithmetic and copies ran while one was open for 15% of the time, Pallas kernels for 0%

commit v1 on v0

v1 whole, which is shorter than its diff:
```python
import functools

import jax
import jax.numpy as jnp
from jax import lax
from jax.experimental import pallas as pl
from jax.experimental.pallas import tpu as pltpu
from jax.sharding import PartitionSpec as P

MESH = pl.DeviceIdType.MESH
F32, BF16 = jnp.float32, jnp.bfloat16

M, D, F = 2048, 2048, 512
HALF = D // 2
W = D // 8
R = 64
S = M // R
TB = 256
NB = M // TB
LAG = 2
NS = 4

A1, A2, A3, B1, B2, B3, FAO, FAY, FBO, FBI, FB2, FD = range(12)
KINDS = 12
NT = (((1,), (1,)), ((), ()))
NN = (((1,), (0,)), ((), ()))


def dot(a, b, dims):
    return lax.dot_general(a, b, dims, preferred_element_type=F32)


def kernel(x_hbm, dy_hbm, gate_hbm, up_hbm, wg_hbm, wu_hbm, wd_hbm, dx_hbm, dwg_hbm, dwu_hbm, dwd_hbm,
           own, fin, term_r, ra1, ra2, ra3, rb1, rb2, rb3, term_s, sa1, sa2, sa3, sb1, sb2, sb3,
           wgu, wd, dyb, gb, ub, dgu, hid_t, tile, tile_t, dwb, dwdb,
           send, recv, tsend, trecv, wsem, bsem, tilesem, osem, dsem):
    me = lax.axis_index("tp")
    c, z, y = lax.rem(me, 2), lax.rem(me // 2, 4), me // 8
    at = lambda yy, zz, cc: (yy * 4 + zz) * 2 + cc
    mate = at(y, z, 1 - c)
    across = at(1 - y, z, c)
    inner = jnp.logical_or(z == 1, z == 2)
    outer = jnp.logical_not(inner)
    right_half = z // 2
    near = at(y, jnp.where(z == 0, 1, jnp.where(z == 1, 0, jnp.where(z == 2, 3, 2))), c)
    far = at(y, jnp.where(z == 1, 2, 1), c)
    root = right_half

    barrier = pltpu.get_barrier_semaphore()
    for peer in (mate, across, near):
        pl.semaphore_signal(barrier, inc=1, device_id={"tp": peer}, device_id_type=MESH)

    @pl.when(inner)
    def _():
        pl.semaphore_signal(barrier, inc=1, device_id={"tp": far}, device_id_type=MESH)

    wcopies = [
        pltpu.make_async_copy(wd_hbm, wd, wsem.at[0]),
        pltpu.make_async_copy(wg_hbm, wgu.at[:, pl.ds(0, F)], wsem.at[1]),
        pltpu.make_async_copy(wu_hbm, wgu.at[:, pl.ds(F, F)], wsem.at[2]),
    ]

    def block_copies(b):
        slot, rows = lax.rem(b, 2), pl.ds(b * TB, TB)
        return [
            pltpu.make_async_copy(dy_hbm.at[rows, :], dyb.at[slot], bsem.at[slot, 0]),
            pltpu.make_async_copy(gate_hbm.at[rows, :], gb.at[slot], bsem.at[slot, 1]),
            pltpu.make_async_copy(up_hbm.at[rows, :], ub.at[slot], bsem.at[slot, 2]),
        ]

    def tile_copy(ref, i):
        slot = lax.rem(i, 2)
        return pltpu.make_async_copy(ref.at[:, pl.ds(i * TB, TB)], tile.at[slot], tilesem.at[slot])

    wcopies[0].start()
    for copy in block_copies(0):
        copy.start()
    wcopies[1].start()
    wcopies[2].start()
    for copy in block_copies(1):
        copy.start()
    tile_copy(x_hbm, 0).start()
    tile_copy(x_hbm, 1).start()

    @pl.when(inner)
    def _():
        pl.semaphore_wait(barrier, 4)

    @pl.when(outer)
    def _():
        pl.semaphore_wait(barrier, 3)

    def term_copy(b):
        slot, rows = lax.rem(b, 2), pl.ds(b * TB, TB)
        return pltpu.make_async_remote_copy(
            term_s.at[slot], term_r.at[rows, :], tsend.at[slot], trecv.at[b],
            device_id={"tp": mate}, device_id_type=MESH)

    def terms(b):
        slot = lax.rem(b, 2)
        row = pl.multiple_of(b * TB, TB)
        rows = pl.ds(row, TB)

        @pl.when(b == 0)
        def _():
            wcopies[0].wait()

        for copy in block_copies(b):
            copy.wait()
        for n in range(F // 256):
            cols = slice(n * 256, (n + 1) * 256)
            dh = dot(dyb[slot], wd[cols, :], NT)
            g, u = gb[slot, :, cols].astype(F32), ub[slot, :, cols].astype(F32)
            sig = 1.0 / (1.0 + jnp.exp(-g))
            silu = g * sig
            du = dh * u
            dgu[rows, cols] = (du * sig + du * g * (sig * (1.0 - sig))).astype(BF16)
            dgu[rows, F + n * 256:F + (n + 1) * 256] = (dh * silu).astype(BF16)
            hid_t[cols, rows] = (silu * u).T.astype(BF16)

        @pl.when(b + 2 < NB)
        def _():
            for copy in block_copies(b + 2):
                copy.start()

        @pl.when(b == 0)
        def _():
            wcopies[1].wait()
            wcopies[2].wait()

        @pl.when(b >= 2)
        def _():
            term_copy(b - 2).wait_send()

        for n in range(HALF // 256):
            t = dot(dgu[rows, :], wgu[pl.ds(pl.multiple_of((1 - c) * HALF + n * 256, 256), 256), :], NT)
            term_s[slot, :, n * 256:(n + 1) * 256] = t.astype(BF16)
        term_copy(b).start()
        for n in range(HALF // 256):
            t = dot(dgu[rows, :], wgu[pl.ds(pl.multiple_of(c * HALF + n * 256, 256), 256), :], NT)
            own[rows, n * 256:(n + 1) * 256] = t

    def dw_copies(i):
        slot, rows = lax.rem(i, 2), pl.ds(i * TB, TB)
        return [
            pltpu.make_async_copy(dwb.at[slot, :, pl.ds(0, F)], dwg_hbm.at[rows, :], dsem.at[slot, 0]),
            pltpu.make_async_copy(dwb.at[slot, :, pl.ds(F, F)], dwu_hbm.at[rows, :], dsem.at[slot, 1]),
        ]

    def dw_gate_up(i):
        slot = lax.rem(i, 2)
        tile_copy(x_hbm, i).wait()
        for j in range(M // 256):
            tile_t[:, j * 256:(j + 1) * 256] = tile[slot, j * 256:(j + 1) * 256, :].T

        @pl.when(i + 2 < NB)
        def _():
            tile_copy(x_hbm, i + 2).start()

        @pl.when(i + 2 >= NB)
        def _():
            tile_copy(dy_hbm, i + 2 - NB).start()

        @pl.when(i >= 2)
        def _():
            for copy in dw_copies(i - 2):
                copy.wait()

        for n in range(2 * F // 256):
            dwb[slot, :, n * 256:(n + 1) * 256] = dot(tile_t[...], dgu[:, n * 256:(n + 1) * 256], NN).astype(BF16)
        for copy in dw_copies(i):
            copy.start()

    def dwd_copy(i):
        slot = lax.rem(i, 2)
        return pltpu.make_async_copy(dwdb.at[slot], dwd_hbm.at[:, pl.ds(i * TB, TB)], dsem.at[slot, 2])

    def dw_down(i):
        slot = lax.rem(i, 2)
        tile_copy(dy_hbm, i).wait()

        @pl.when(i >= 2)
        def _():
            dwd_copy(i - 2).wait()

        for n in range(F // 256):
            dwdb[slot, n * 256:(n + 1) * 256, :] = dot(hid_t[n * 256:(n + 1) * 256, :], tile[slot], NN).astype(BF16)

        @pl.when(i + 2 < NB)
        def _():
            tile_copy(dy_hbm, i + 2).start()

        dwd_copy(i).start()

    def part(ref, k, col=0, width=W):
        return ref.at[pl.ds(pl.multiple_of(k * R, R), R), pl.ds(col, width)]

    base = pl.multiple_of(c * HALF, HALF)
    col_a = pl.multiple_of(y * W, W)
    col_a_other = pl.multiple_of((1 - y) * W, W)
    col_b = pl.multiple_of(2 * W + root * W, W)
    col_b_other = pl.multiple_of(2 * W + (1 - root) * W, W)

    def message(kind, k, there=False):
        slot = lax.rem(k, NS)
        fin_own = lambda col, width=W: part(fin, k, pl.multiple_of(base + col, W), width)
        a_col = col_a_other if there else col_a
        src, dst, peer = {
            A1: (sa1.at[slot], part(ra1, k), across),
            A2: (sa2.at[slot], part(ra2, k), near),
            A3: (sa3.at[slot], part(ra3, k), far),
            B1: (sb1.at[slot], part(rb1, k, 0, 2 * W), near),
            B2: (sb2.at[slot], part(rb2, k), far),
            B3: (sb3.at[slot], part(rb3, k), across),
            FAO: (fin_own(col_a), fin_own(col_a), near),
            FAY: (fin_own(a_col), fin_own(a_col), across),
            FBO: (fin_own(col_b), fin_own(col_b), near),
            FBI: (fin_own(col_b_other if there else col_b), fin_own(col_b_other if there else col_b), far),
            FB2: (fin_own(col_b_other), fin_own(col_b_other), near),
            FD: None,
        }[kind] or (None, None, None)
        if kind == FD:
            col = pl.multiple_of((1 - c) * HALF if there else c * HALF, HALF)
            src = dst = part(fin, k, col, HALF)
            peer = mate
        return pltpu.make_async_remote_copy(
            src, dst, send.at[kind, slot], recv.at[kind, k], device_id={"tp": peer}, device_id_type=MESH)

    def free(kind, k):
        @pl.when(k >= NS)
        def _():
            message(kind, k - NS).wait_send()

    def arrived(kind, k):
        message(kind, k, there=True).wait_recv()

    def ld(ref, k, col=0, width=W):
        return ref[pl.ds(pl.multiple_of(k * R, R), R), pl.ds(col, width)].astype(F32)

    def st(ref, k, col, value, width=W):
        ref[pl.ds(pl.multiple_of(k * R, R), R), pl.ds(col, width)] = value

    def e1(k):
        @pl.when(lax.rem(k, TB // R) == 0)
        def _():
            term_copy(k // (TB // R)).wait_recv()

        slot = lax.rem(k, NS)
        free(A1, k)
        sa1[slot] = (ld(own, k, col_a_other) + ld(term_r, k, col_a_other)).astype(BF16)
        message(A1, k).start()

        @pl.when(outer)
        def _():
            free(B1, k)
            sb1[slot] = (ld(own, k, 2 * W, 2 * W) + ld(term_r, k, 2 * W, 2 * W)).astype(BF16)
            message(B1, k).start()

        @pl.when(inner)
        def _():
            st(own, k, 2 * W, ld(own, k, 2 * W, 2 * W) + ld(term_r, k, 2 * W, 2 * W), 2 * W)

        st(own, k, col_a, ld(own, k, col_a) + ld(term_r, k, col_a))

    def e2(k):
        slot = lax.rem(k, NS)

        @pl.when(inner)
        def _():
            arrived(B1, k)
            free(B2, k)
            other = pl.multiple_of((1 - root) * W, W)
            sb2[slot] = (ld(own, k, col_b_other) + ld(rb1, k, other)).astype(BF16)
            message(B2, k).start()
            st(own, k, col_b, ld(own, k, col_b) + ld(rb1, k, pl.multiple_of(root * W, W)))

        arrived(A1, k)

        @pl.when(outer)
        def _():
            free(A2, k)
            sa2[slot] = (ld(own, k, col_a) + ld(ra1, k)).astype(BF16)
            message(A2, k).start()

        @pl.when(inner)
        def _():
            st(own, k, col_a, ld(own, k, col_a) + ld(ra1, k))

    def e3(k):
        slot = lax.rem(k, NS)

        @pl.when(inner)
        def _():
            arrived(B2, k)
            free(B3, k)
            sb3[slot] = (ld(own, k, col_b) + ld(rb2, k)).astype(BF16)
            message(B3, k).start()
            arrived(A2, k)
            free(A3, k)
            sa3[slot] = (ld(own, k, col_a) + ld(ra2, k)).astype(BF16)
            message(A3, k).start()

    def e4(k):
        slot = lax.rem(k, NS)

        @pl.when(inner)
        def _():
            arrived(B3, k)
            st(fin, k, pl.multiple_of(base + col_b, W), (sb3[slot].astype(F32) + ld(rb3, k)).astype(BF16))
            free(FBI, k)
            message(FBI, k).start()
            free(FBO, k)
            message(FBO, k).start()
            arrived(A3, k)
            st(fin, k, pl.multiple_of(base + col_a, W), (sa3[slot].astype(F32) + ld(ra3, k)).astype(BF16))
            free(FAO, k)
            message(FAO, k).start()
            free(FAY, k)
            message(FAY, k).start()

    def e5(k):
        @pl.when(inner)
        def _():
            arrived(FBI, k)
            free(FB2, k)
            message(FB2, k).start()

        @pl.when(outer)
        def _():
            arrived(FAO, k)
            free(FAY, k)
            message(FAY, k).start()

    def e6(k):
        @pl.when(outer)
        def _():
            arrived(FBO, k)
            arrived(FB2, k)

        arrived(FAY, k)
        free(FD, k)
        message(FD, k).start()

    def out_copy(k):
        rows = pl.ds(pl.multiple_of(k * R, R), R)
        return pltpu.make_async_copy(fin.at[rows, :], dx_hbm.at[rows, :], osem.at[lax.rem(k, NS)])

    def e7(k):
        arrived(FD, k)

        @pl.when(k >= NS)
        def _():
            out_copy(k - NS).wait()

        out_copy(k).start()

    events = [(e1, 1), (e2, 1 + LAG), (e3, 1 + 2 * LAG), (e4, 1 + 3 * LAG), (e5, 1 + 4 * LAG), (e6, 1 + 5 * LAG), (e7, 2 + 5 * LAG)]
    steps = S + 2 + 5 * LAG

    def step(s, _):
        for event, offset in events:
            @pl.when(jnp.logical_and(s >= offset, s < S + offset))
            def _(event=event, offset=offset):
                event(s - offset)

        @pl.when(jnp.logical_and(lax.rem(s, 2) == 0, s < 2 * NB))
        def _():
            terms(s // 2)

        @pl.when(jnp.logical_and(s >= 2 * NB, s < 3 * NB))
        def _():
            dw_gate_up(s - 2 * NB)

        @pl.when(jnp.logical_and(s >= 3 * NB, s < 4 * NB))
        def _():
            dw_down(s - 3 * NB)

        return 0

    lax.fori_loop(0, steps, step, 0)

    for b in (NB - 2, NB - 1):
        term_copy(b).wait_send()
        for copy in dw_copies(b):
            copy.wait()
        dwd_copy(b).wait()

    def drain(kinds):
        for kind in kinds:
            for k in range(S - NS, S):
                message(kind, k).wait_send()

    drain((A1, FAY, FD))

    @pl.when(inner)
    def _():
        drain((A3, B2, B3, FAO, FBO, FBI, FB2))

    @pl.when(outer)
    def _():
        drain((A2, B1))

    for k in range(S - NS, S):
        out_copy(k).wait()


def solution(mesh):
    def step(x, dy, gate, up, w_gate, w_up, w_down):
        vmem = pltpu.VMEM
        dma = pltpu.SemaphoreType.DMA
        scratch = [
            vmem((M, HALF), F32), vmem((M, D), BF16), vmem((M, HALF), BF16),
            vmem((M, W), BF16), vmem((M, W), BF16), vmem((M, W), BF16),
            vmem((M, 2 * W), BF16), vmem((M, W), BF16), vmem((M, W), BF16),
            vmem((2, TB, HALF), BF16),
            vmem((NS, R, W), BF16), vmem((NS, R, W), BF16), vmem((NS, R, W), BF16),
            vmem((NS, R, 2 * W), BF16), vmem((NS, R, W), BF16), vmem((NS, R, W), BF16),
            vmem((D, 2 * F), BF16), vmem((F, D), BF16),
            vmem((2, TB, D), BF16), vmem((2, TB, F), BF16), vmem((2, TB, F), BF16),
            vmem((M, 2 * F), BF16), vmem((F, M), BF16),
            vmem((2, M, TB), BF16), vmem((TB, M), BF16), vmem((2, TB, 2 * F), BF16), vmem((2, F, TB), BF16),
            dma((KINDS, NS)), dma((KINDS, S)), dma((2,)), dma((NB,)), dma((3,)), dma((2, 3)), dma((2,)), dma((NS,)), dma((2, 3)),
        ]
        anywhere = pl.BlockSpec(memory_space=pl.ANY)
        shape = jax.ShapeDtypeStruct
        return pl.pallas_call(
            kernel,
            out_shape=(shape((M, D), BF16), shape((D, F), BF16), shape((D, F), BF16), shape((F, D), BF16)),
            in_specs=[anywhere] * 7,
            out_specs=(anywhere,) * 4,
            scratch_shapes=scratch,
            compiler_params=pltpu.CompilerParams(collective_id=0, has_side_effects=True, vmem_limit_bytes=64 * 1024 * 1024 - 65536),
        )(x, dy, gate, up, w_gate, w_up, w_down)

    tokens, columns, rows = P("dp", None), P(None, "tp"), P("tp", None)
    return jax.shard_map(
        step,
        mesh=mesh,
        in_specs=(tokens, tokens, P("dp", "tp"), P("dp", "tp"), columns, columns, rows),
        out_specs=(tokens, P("dp", "tp"), P("dp", "tp"), P(("dp", "tp"), None)),
        check_vma=False,
    )
```

time: 234 us -> 116 us (0.50)
  waiting for transfers between devices: 138 us -> 0 us
  Pallas kernels: 0 us -> 99.9 us
  matrix products: 68 us -> 0 us
  between operations: 14.1 us -> 0.65 us
    psum x1 -> x0, waiting for transfers between devices: 138 us -> none  [step(): dx = lax.psum(term.astype(jnp.bfloat16), 'tp')]
    pallas_call x0 -> x1, Pallas kernels: none -> 99.9 us  [step(): pl.pallas_call(kernel, out_shape=(shape((M, D), BF16), shape((D, F), BF16...]
    dot_general x6 -> x0, matrix products: 68 us -> none  [the longest x1 16.5 us: step(): jnp.dot(d_up, w_up.T, preferred_element_type=jnp.float32)]
    unnamed x9 -> x10, local copies, waits for them, and re-layouts: 13.6 us -> 14.6 us
  transfers between devices with their start and end apart: 1 -> 0, of which waited for: 1 -> 0; matrix products, arithmetic and copies ran while one was open for 15% -> 0% of each run, Pallas kernels for 0% -> 0%
where the time goes in v1:
time: 116 us; the launch traced here: 115 us
  Pallas kernels  99.9 us (86%)
  local copies, waits for them, and re-layouts  14.6 us (13%)
    pallas_call x1, Pallas kernels, step(): pl.pallas_call(kernel, out_shape=(shape((M, D), BF16), shape((D, F), BF16...  99.9 us
    unnamed x10, local copies, waits for them, and re-layouts  14.6 us

profile of v1, /device:TPU:0, one launch (start us, length us, event | category | flops | bytes accessed | tf_op | source)
XLA Modules:
  0.0 115.1 jit_solution(8426331610927094460)
XLA Ops:
  0.6 99.9 %shard_map.102 = (bf16[2048,2048]{1,0:T(8,128)(2,1)}, bf16[2048,512]{1,0:T(8,128)(2,1)}, bf16[2048,512]{1,0:T(8,128)(2,1)}, bf16[512,2048]{1,0:T(8,128)(2,1)}) custom-call(bf16[2048,2048]{1,0:T(8,128)(2,1)} %x_hbm.1, bf16[2048,2048]{1,0:T(8,128)(2,1)} %dy_hbm.1, bf16[2048,512]{1,0:T(8,128)(2,1)} %gate_hbm.1, bf16[2048,512]{1,0:T(8,128)(2,1)} %up_hbm.1, ...), custom_call_target="tpu_custom_call" | custom-call | tf_op jit(solution)/shard_map/pallas_call | solution.py:426
  100.5 0.0 copy-start.2
  100.5 8.6 %copy.15 = bf16[2048,2048]{1,0:T(8,128)(2,1)} copy(bf16[2048,2048]{1,0:T(8,128)(2,1)} %get-tuple-element.8) | data formatting | bytes 16777216
  109.1 0.0 copy-done.2
  109.1 0.0 copy-start.1
  109.1 1.3 %copy.16 = bf16[2048,512]{1,0:T(8,128)(2,1)} copy(bf16[2048,512]{1,0:T(8,128)(2,1)S(1)} %copy-done.2) | data formatting | bytes 4194304
  110.4 1.0 copy-done.1
  111.4 0.0 copy-start
  111.4 1.3 %copy.17 = bf16[2048,512]{1,0:T(8,128)(2,1)} copy(bf16[2048,512]{1,0:T(8,128)(2,1)S(1)} %copy-done.1) | data formatting | bytes 4194304
  112.8 1.0 copy-done
  113.8 1.3 %copy.18 = bf16[512,2048]{1,0:T(8,128)(2,1)} copy(bf16[512,2048]{1,0:T(8,128)(2,1)S(1)} %copy-done) | data formatting | bytes 4194304
Async XLA Ops:
  100.5 8.6 %copy-start.2 = (bf16[2048,512]{1,0:T(8,128)(2,1)S(1)}, bf16[2048,512]{1,0:T(8,128)(2,1)}, u32[]{:S(2)}) copy-start(bf16[2048,512]{1,0:T(8,128)(2,1)} %get-tuple-element.9) | copy-start | bytes 6291460
  109.1 2.3 %copy-start.1 = (bf16[2048,512]{1,0:T(8,128)(2,1)S(1)}, bf16[2048,512]{1,0:T(8,128)(2,1)}, u32[]{:S(2)}) copy-start(bf16[2048,512]{1,0:T(8,128)(2,1)} %get-tuple-element.10) | copy-start | bytes 6291460
  111.4 2.3 %copy-start = (bf16[512,2048]{1,0:T(8,128)(2,1)S(1)}, bf16[512,2048]{1,0:T(8,128)(2,1)}, u32[]{:S(2)}) copy-start(bf16[512,2048]{1,0:T(8,128)(2,1)} %get-tuple-element.11) | copy-start | bytes 6291460

commit v2 on v1

--- a/solution.py
+++ b/solution.py
@@ -19,6 +19,7 @@
 NB = M // TB
 LAG = 2
 NS = 4
+LIMIT = 48 * 1024 * 1024
 
 A1, A2, A3, B1, B2, B3, FAO, FAY, FBO, FBI, FB2, FD = range(12)
 KINDS = 12
@@ -30,10 +31,10 @@
     return lax.dot_general(a, b, dims, preferred_element_type=F32)
 
 
-def kernel(x_hbm, dy_hbm, gate_hbm, up_hbm, wg_hbm, wu_hbm, wd_hbm, dx_hbm, dwg_hbm, dwu_hbm, dwd_hbm,
-           own, fin, term_r, ra1, ra2, ra3, rb1, rb2, rb3, term_s, sa1, sa2, sa3, sb1, sb2, sb3,
-           wgu, wd, dyb, gb, ub, dgu, hid_t, tile, tile_t, dwb, dwdb,
-           send, recv, tsend, trecv, wsem, bsem, tilesem, osem, dsem):
+def kernel(x_hbm, dy_hbm, gate_hbm, up_hbm, wg_hbm, wu_hbm, wd_hbm, fin, dwg, dwu, dwd,
+           own, term_r, ra1, ra2, ra3, rb1, rb2, rb3, term_s, sa1, sa2, sa3, sb1, sb2, sb3,
+           wgu, wd, dyb, gb, ub, dgu, hid_t, tile, tile_t,
+           send, recv, tsend, trecv, wsem, bsem, tilesem):
     me = lax.axis_index("tp")
     c, z, y = lax.rem(me, 2), lax.rem(me // 2, 4), me // 8
     at = lambda yy, zz, cc: (yy * 4 + zz) * 2 + cc
@@ -140,13 +141,6 @@
             t = dot(dgu[rows, :], wgu[pl.ds(pl.multiple_of(c * HALF + n * 256, 256), 256), :], NT)
             own[rows, n * 256:(n + 1) * 256] = t
 
-    def dw_copies(i):
-        slot, rows = lax.rem(i, 2), pl.ds(i * TB, TB)
-        return [
-            pltpu.make_async_copy(dwb.at[slot, :, pl.ds(0, F)], dwg_hbm.at[rows, :], dsem.at[slot, 0]),
-            pltpu.make_async_copy(dwb.at[slot, :, pl.ds(F, F)], dwu_hbm.at[rows, :], dsem.at[slot, 1]),
-        ]
-
     def dw_gate_up(i):
         slot = lax.rem(i, 2)
         tile_copy(x_hbm, i).wait()
@@ -161,36 +155,23 @@
         def _():
             tile_copy(dy_hbm, i + 2 - NB).start()
 
-        @pl.when(i >= 2)
-        def _():
-            for copy in dw_copies(i - 2):
-                copy.wait()
-
-        for n in range(2 * F // 256):
-            dwb[slot, :, n * 256:(n + 1) * 256] = dot(tile_t[...], dgu[:, n * 256:(n + 1) * 256], NN).astype(BF16)
-        for copy in dw_copies(i):
-            copy.start()
-
-    def dwd_copy(i):
-        slot = lax.rem(i, 2)
-        return pltpu.make_async_copy(dwdb.at[slot], dwd_hbm.at[:, pl.ds(i * TB, TB)], dsem.at[slot, 2])
+        rows = pl.ds(pl.multiple_of(i * TB, TB), TB)
+        for n in range(F // 256):
+            cols = slice(n * 256, (n + 1) * 256)
+            dwg[rows, cols] = dot(tile_t[...], dgu[:, n * 256:(n + 1) * 256], NN).astype(BF16)
+            dwu[rows, cols] = dot(tile_t[...], dgu[:, F + n * 256:F + (n + 1) * 256], NN).astype(BF16)
 
     def dw_down(i):
         slot = lax.rem(i, 2)
         tile_copy(dy_hbm, i).wait()
 
-        @pl.when(i >= 2)
-        def _():
-            dwd_copy(i - 2).wait()
-
+        cols = pl.ds(pl.multiple_of(i * TB, TB), TB)
         for n in range(F // 256):
-            dwdb[slot, n * 256:(n + 1) * 256, :] = dot(hid_t[n * 256:(n + 1) * 256, :], tile[slot], NN).astype(BF16)
+            dwd[n * 256:(n + 1) * 256, cols] = dot(hid_t[n * 256:(n + 1) * 256, :], tile[slot], NN).astype(BF16)
 
         @pl.when(i + 2 < NB)
         def _():
             tile_copy(dy_hbm, i + 2).start()
-
-        dwd_copy(i).start()
 
     def part(ref, k, col=0, width=W):
         return ref.at[pl.ds(pl.multiple_of(k * R, R), R), pl.ds(col, width)]
@@ -341,18 +322,8 @@
         free(FD, k)
         message(FD, k).start()
 
-    def out_copy(k):
-        rows = pl.ds(pl.multiple_of(k * R, R), R)
-        return pltpu.make_async_copy(fin.at[rows, :], dx_hbm.at[rows, :], osem.at[lax.rem(k, NS)])
-
     def e7(k):
         arrived(FD, k)
-
-        @pl.when(k >= NS)
-        def _():
-            out_copy(k - NS).wait()
-
-        out_copy(k).start()
 
     events = [(e1, 1), (e2, 1 + LAG), (e3, 1 + 2 * LAG), (e4, 1 + 3 * LAG), (e5, 1 + 4 * LAG), (e6, 1 + 5 * LAG), (e7, 2 + 5 * LAG)]
     steps = S + 2 + 5 * LAG
@@ -381,9 +352,6 @@
 
     for b in (NB - 2, NB - 1):
         term_copy(b).wait_send()
-        for copy in dw_copies(b):
-            copy.wait()
-        dwd_copy(b).wait()
 
     def drain(kinds):
         for kind in kinds:
@@ -400,8 +368,22 @@
     def _():
         drain((A2, B1))
 
-    for k in range(S - NS, S):
-        out_copy(k).wait()
+
+PIECES = 4
+
+
+def write_out(*refs):
+    sources, targets, sems = refs[:4], refs[4:8], refs[8]
+    copies = []
+    for i, (source, target) in enumerate(zip(sources, targets)):
+        size = source.shape[0] // PIECES
+        for j in range(PIECES):
+            rows = pl.ds(j * size, size)
+            copies.append(pltpu.make_async_copy(source.at[rows, :], target.at[rows, :], sems.at[i, j]))
+    for copy in copies:
+        copy.start()
+    for copy in copies:
+        copy.wait()
 
 
 def solution(mesh):
@@ -409,7 +391,7 @@
         vmem = pltpu.VMEM
         dma = pltpu.SemaphoreType.DMA
         scratch = [
-            vmem((M, HALF), F32), vmem((M, D), BF16), vmem((M, HALF), BF16),
+            vmem((M, HALF), F32), vmem((M, HALF), BF16),
             vmem((M, W), BF16), vmem((M, W), BF16), vmem((M, W), BF16),
             vmem((M, 2 * W), BF16), vmem((M, W), BF16), vmem((M, W), BF16),
             vmem((2, TB, HALF), BF16),
@@ -418,19 +400,28 @@
             vmem((D, 2 * F), BF16), vmem((F, D), BF16),
             vmem((2, TB, D), BF16), vmem((2, TB, F), BF16), vmem((2, TB, F), BF16),
             vmem((M, 2 * F), BF16), vmem((F, M), BF16),
-            vmem((2, M, TB), BF16), vmem((TB, M), BF16), vmem((2, TB, 2 * F), BF16), vmem((2, F, TB), BF16),
-            dma((KINDS, NS)), dma((KINDS, S)), dma((2,)), dma((NB,)), dma((3,)), dma((2, 3)), dma((2,)), dma((NS,)), dma((2, 3)),
+            vmem((2, M, TB), BF16), vmem((TB, M), BF16),
+            dma((KINDS, NS)), dma((KINDS, S)), dma((2,)), dma((NB,)), dma((3,)), dma((2, 3)), dma((2,)),
         ]
         anywhere = pl.BlockSpec(memory_space=pl.ANY)
         shape = jax.ShapeDtypeStruct
+        shapes = ((M, D), (D, F), (D, F), (F, D))
+        grads = pl.pallas_call(
+            kernel,
+            out_shape=tuple(vmem(dims, BF16) for dims in shapes),
+            in_specs=[anywhere] * 7,
+            out_specs=(pl.BlockSpec(memory_space=vmem),) * 4,
+            scratch_shapes=scratch,
+            compiler_params=pltpu.CompilerParams(collective_id=0, has_side_effects=True, vmem_limit_bytes=LIMIT),
+        )(x, dy, gate, up, w_gate, w_up, w_down)
         return pl.pallas_call(
-            kernel,
-            out_shape=(shape((M, D), BF16), shape((D, F), BF16), shape((D, F), BF16), shape((F, D), BF16)),
-            in_specs=[anywhere] * 7,
+            write_out,
+            out_shape=tuple(shape(dims, BF16) for dims in shapes),
+            in_specs=[pl.BlockSpec(memory_space=vmem)] * 4,
             out_specs=(anywhere,) * 4,
-            scratch_shapes=scratch,
-            compiler_params=pltpu.CompilerParams(collective_id=0, has_side_effects=True, vmem_limit_bytes=64 * 1024 * 1024 - 65536),
-        )(x, dy, gate, up, w_gate, w_up, w_down)
+            scratch_shapes=[dma((4, PIECES))],
+            compiler_params=pltpu.CompilerParams(vmem_limit_bytes=1 << 20),
+        )(*grads)
 
     tokens, columns, rows = P("dp", None), P(None, "tp"), P("tp", None)
     return jax.shard_map(

time: 116 us -> 106 us (0.914)
  local copies, waits for them, and re-layouts: 14.6 us -> 0 us
  Pallas kernels: 99.9 us -> 105 us
    unnamed x10 -> x0, local copies, waits for them, and re-layouts: 14.6 us -> none
    pallas_call x1 -> x2, Pallas kernels: 99.9 us -> 105 us  [the longest x1 99.7 us: step(): pl.pallas_call(kernel, out_shape=tuple((vmem(dims, BF16) for dims in shap...]
where the time goes in v2:
time: 106 us
  Pallas kernels  105 us (99%)
    pallas_call x1, Pallas kernels, step(): pl.pallas_call(kernel, out_shape=tuple((vmem(dims, BF16) for dims in shap...  99.7 us
    pallas_call x1, Pallas kernels, step(): pl.pallas_call(write_out, out_shape=tuple((shape(dims, BF16) for dims in...  5.31 us

profile of v2, /device:TPU:0, one launch (start us, length us, event | category | flops | bytes accessed | tf_op | source)
XLA Modules:
  0.0 105.6 jit_solution(6597250195985640870)
XLA Ops:
  0.6 99.7 %shard_map.102 = (bf16[2048,2048]{1,0:T(8,128)(2,1)S(1)}, bf16[2048,512]{1,0:T(8,128)(2,1)S(1)}, bf16[2048,512]{1,0:T(8,128)(2,1)S(1)}, bf16[512,2048]{1,0:T(8,128)(2,1)S(1)}) custom-call(bf16[2048,2048]{1,0:T(8,128)(2,1)} %x_hbm.1, bf16[2048,2048]{1,0:T(8,128)(2,1)} %dy_hbm.1, bf16[2048,512]{1,0:T(8,128)(2,1)} %gate_hbm.1, bf16[2048,512]{1,0:T(8,128)(2,1)} %up_hbm.1, ...), custom_call_target="tpu_custom_call" | custom-call | tf_op jit(solution)/shard_map/pallas_call | solution.py:409
  100.3 5.3 %shard_map.103 = (bf16[2048,2048]{1,0:T(8,128)(2,1)}, bf16[2048,512]{1,0:T(8,128)(2,1)}, bf16[2048,512]{1,0:T(8,128)(2,1)}, bf16[512,2048]{1,0:T(8,128)(2,1)}) custom-call(bf16[2048,2048]{1,0:T(8,128)(2,1)S(1)} %get-tuple-element.8.refs_0_, bf16[2048,512]{1,0:T(8,128)(2,1)S(1)} %get-tuple-element.9.refs_1_, bf16[2048,512]{1,0:T(8,128)(2,1)S(1)} %get-tuple-element.10.refs_2_, ...), custom_call_target="tpu_custom_call" | custom-call | tf_op jit(solution)/shard_map/pallas_call | solution.py:417

commit v3 on v2

--- a/solution.py
+++ b/solution.py
@@ -12,17 +12,23 @@
 
 M, D, F = 2048, 2048, 512
 HALF = D // 2
-W = D // 8
+WA, WB = 640, 384
 R = 64
+H = R // 2
 S = M // R
 TB = 256
 NB = M // TB
-LAG = 2
+A_AT = (1, 5, 7, 9, 13, 18)
+B_AT = (3, 5, 7, 10, 12, 16)
+C_AT = (1, 3, 5, 8, 10, 12, 14, 18)
 NS = 4
 LIMIT = 48 * 1024 * 1024
 
-A1, A2, A3, B1, B2, B3, FAO, FAY, FBO, FBI, FB2, FD = range(12)
-KINDS = 12
+A1, A2, A3, FAO, FAY, B1, B2, B3, FBO, FBI, FB2, C1, C2, C3, C4, FC1, FC2, FC3, FDA, FDB = range(20)
+ROW = {kind: row for row, kinds in enumerate((
+    (A1,), (A2,), (A3,), (FAO,), (FAY,), (B1, C1), (B2, C2), (B3, C3), (FBO, C4), (FBI, FC2), (FB2, FC3), (FC1,), (FDA,), (FDB,)
+)) for kind in kinds}
+ROWS = 14
 NT = (((1,), (1,)), ((), ()))
 NN = (((1,), (0,)), ((), ()))
 
@@ -32,7 +38,7 @@
 
 
 def kernel(x_hbm, dy_hbm, gate_hbm, up_hbm, wg_hbm, wu_hbm, wd_hbm, fin, dwg, dwu, dwd,
-           own, term_r, ra1, ra2, ra3, rb1, rb2, rb3, term_s, sa1, sa2, sa3, sb1, sb2, sb3,
+           own, term_r, ra1, ra2, ra3, rb1, rb2, rb3, rb4, term_s, sa1, sa2, sa3, sb1, sb2, sb3, sb4,
            wgu, wd, dyb, gb, ub, dgu, hid_t, tile, tile_t,
            send, recv, tsend, trecv, wsem, bsem, tilesem):
     me = lax.axis_index("tp")
@@ -173,166 +179,257 @@
         def _():
             tile_copy(dy_hbm, i + 2).start()
 
-    def part(ref, k, col=0, width=W):
-        return ref.at[pl.ds(pl.multiple_of(k * R, R), R), pl.ds(col, width)]
-
     base = pl.multiple_of(c * HALF, HALF)
-    col_a = pl.multiple_of(y * W, W)
-    col_a_other = pl.multiple_of((1 - y) * W, W)
-    col_b = pl.multiple_of(2 * W + root * W, W)
-    col_b_other = pl.multiple_of(2 * W + (1 - root) * W, W)
+    side, off_side = root, 1 - root
+
+    def rows_of(k, half=None):
+        if half is None:
+            return pl.ds(pl.multiple_of(k * R, R), R)
+        return pl.ds(pl.multiple_of(k * R + half * H, H), H)
+
+    def got(ref, k):
+        return ref.at[pl.ds(pl.multiple_of(k * H, H), H), :]
+
+    def pair(ref, k):
+        return ref.at[pl.ds(pl.multiple_of(k // 2 * H, H), H), :]
+
+    def whole(ref, k):
+        return ref.at[pl.ds(pl.multiple_of(k // 2 * R, R), R), :]
+
+    def final(k, half, col, width, core=None):
+        start = pl.multiple_of((base if core is None else core) + col, 128)
+        return fin.at[rows_of(k, half), pl.ds(start, width)]
 
     def message(kind, k, there=False):
         slot = lax.rem(k, NS)
-        fin_own = lambda col, width=W: part(fin, k, pl.multiple_of(base + col, W), width)
-        a_col = col_a_other if there else col_a
-        src, dst, peer = {
-            A1: (sa1.at[slot], part(ra1, k), across),
-            A2: (sa2.at[slot], part(ra2, k), near),
-            A3: (sa3.at[slot], part(ra3, k), far),
-            B1: (sb1.at[slot], part(rb1, k, 0, 2 * W), near),
-            B2: (sb2.at[slot], part(rb2, k), far),
-            B3: (sb3.at[slot], part(rb3, k), across),
-            FAO: (fin_own(col_a), fin_own(col_a), near),
-            FAY: (fin_own(a_col), fin_own(a_col), across),
-            FBO: (fin_own(col_b), fin_own(col_b), near),
-            FBI: (fin_own(col_b_other if there else col_b), fin_own(col_b_other if there else col_b), far),
-            FB2: (fin_own(col_b_other), fin_own(col_b_other), near),
-            FD: None,
-        }[kind] or (None, None, None)
-        if kind == FD:
-            col = pl.multiple_of((1 - c) * HALF if there else c * HALF, HALF)
-            src = dst = part(fin, k, col, HALF)
+        if kind in (A1, A2, A3):
+            src, dst, peer = {A1: (sa1, ra1, across), A2: (sa2, ra2, near), A3: (sa3, ra3, far)}[kind]
+            src, dst = src.at[slot], got(dst, k)
+        elif kind == B1:
+            src, dst, peer = sb1.at[slot], whole(rb1, k), near
+        elif kind in (C1, B2, C2, B3, C3, C4):
+            src, dst, peer = {
+                C1: (sb2, rb4, near), B2: (sb2, rb2, far), C2: (sb2, rb2, far), B3: (sb3, rb3, across), C3: (sb3, rb3, near),
+                C4: (sb4, rb4, across)}[kind]
+            src, dst = src.at[slot], (got if kind in (B2, C2, B3, C3) else pair)(dst, k)
+        elif kind in (FDA, FDB):
+            core = pl.multiple_of((1 - c) * HALF if there else c * HALF, HALF)
+            src = dst = final(k, None, *((0, WA) if kind == FDA else (WA, WB)), core=core)
             peer = mate
+        else:
+            mine, theirs, col, width, peer = {
+                FAO: (y, y, 0, WA, near), FAY: (y, 1 - y, 0, WA, across),
+                FBO: (side, side, WA, WB, near), FBI: (side, off_side, WA, WB, far), FB2: (off_side, off_side, WA, WB, near),
+                FC1: (side, side, WA, WB, near), FC2: (side, off_side, WA, WB, far), FC3: (off_side, off_side, WA, WB, near),
+            }[kind]
+            src = dst = final(k, theirs if there else mine, col, width)
+        row = ROW[kind]
         return pltpu.make_async_remote_copy(
-            src, dst, send.at[kind, slot], recv.at[kind, k], device_id={"tp": peer}, device_id_type=MESH)
+            src, dst, send.at[row, slot], recv.at[row, k], device_id={"tp": peer}, device_id_type=MESH)
+
+    def go(kind, k):
+        message(kind, k).start()
 
     def free(kind, k):
         @pl.when(k >= NS)
         def _():
             message(kind, k - NS).wait_send()
 
+    def pass_on(kind, k):
+        free(kind, k)
+        go(kind, k)
+
     def arrived(kind, k):
         message(kind, k, there=True).wait_recv()
 
-    def ld(ref, k, col=0, width=W):
-        return ref[pl.ds(pl.multiple_of(k * R, R), R), pl.ds(col, width)].astype(F32)
-
-    def st(ref, k, col, value, width=W):
-        ref[pl.ds(pl.multiple_of(k * R, R), R), pl.ds(col, width)] = value
-
-    def e1(k):
+    def mine_of(k, half, col, width):
+        return own[rows_of(k, half), col:col + width]
+
+    def with_mate(k, half, col, width):
+        return mine_of(k, half, col, width) + term_r[rows_of(k, half), col:col + width].astype(F32)
+
+    def keep(k, half, col, width, value):
+        own[rows_of(k, half), col:col + width] = value
+
+    def send_sum(kind, ref, k, value):
+        free(kind, k)
+        ref[lax.rem(k, NS)] = value.astype(BF16)
+        go(kind, k)
+
+    def put_final(k, half, col, width, sent, received):
+        final(k, half, col, width)[...] = (sent[lax.rem(k, NS)].astype(F32) + received[...].astype(F32)).astype(BF16)
+
+    on_inner, on_outer = pl.when(inner), pl.when(outer)
+
+    def a1(k):
         @pl.when(lax.rem(k, TB // R) == 0)
         def _():
             term_copy(k // (TB // R)).wait_recv()
 
-        slot = lax.rem(k, NS)
-        free(A1, k)
-        sa1[slot] = (ld(own, k, col_a_other) + ld(term_r, k, col_a_other)).astype(BF16)
-        message(A1, k).start()
-
-        @pl.when(outer)
-        def _():
-            free(B1, k)
-            sb1[slot] = (ld(own, k, 2 * W, 2 * W) + ld(term_r, k, 2 * W, 2 * W)).astype(BF16)
-            message(B1, k).start()
-
-        @pl.when(inner)
-        def _():
-            st(own, k, 2 * W, ld(own, k, 2 * W, 2 * W) + ld(term_r, k, 2 * W, 2 * W), 2 * W)
-
-        st(own, k, col_a, ld(own, k, col_a) + ld(term_r, k, col_a))
-
-    def e2(k):
-        slot = lax.rem(k, NS)
-
-        @pl.when(inner)
+        send_sum(A1, sa1, k, with_mate(k, 1 - y, 0, WA))
+        keep(k, y, 0, WA, with_mate(k, y, 0, WA))
+
+    def a2(k):
+        arrived(A1, k)
+
+        @on_outer
+        def _():
+            send_sum(A2, sa2, k, mine_of(k, y, 0, WA) + got(ra1, k)[...].astype(F32))
+
+        @on_inner
+        def _():
+            keep(k, y, 0, WA, mine_of(k, y, 0, WA) + got(ra1, k)[...].astype(F32))
+
+    def a3(k):
+        @on_inner
+        def _():
+            arrived(A2, k)
+            send_sum(A3, sa3, k, mine_of(k, y, 0, WA) + got(ra2, k)[...].astype(F32))
+
+    def a4(k):
+        @on_inner
+        def _():
+            arrived(A3, k)
+            put_final(k, y, 0, WA, sa3, got(ra3, k))
+            pass_on(FAO, k)
+            pass_on(FAY, k)
+
+    def a5(k):
+        @on_inner
+        def _():
+            arrived(FAY, k)
+            pass_on(FDA, k)
+
+        @on_outer
+        def _():
+            arrived(FAO, k)
+            pass_on(FAY, k)
+
+    def a6(k):
+        @on_outer
+        def _():
+            arrived(FAY, k)
+            pass_on(FDA, k)
+
+    def b1(k):
+        @on_outer
+        def _():
+            send_sum(B1, sb1, k, with_mate(k, None, WA, WB))
+
+        @on_inner
+        def _():
+            keep(k, None, WA, WB, with_mate(k, None, WA, WB))
+
+    def half_of(ref, k, half):
+        return ref[pl.ds(pl.multiple_of(k // 2 * R + half * H, H), H), :].astype(F32)
+
+    def b2(k):
+        @on_inner
         def _():
             arrived(B1, k)
-            free(B2, k)
-            other = pl.multiple_of((1 - root) * W, W)
-            sb2[slot] = (ld(own, k, col_b_other) + ld(rb1, k, other)).astype(BF16)
-            message(B2, k).start()
-            st(own, k, col_b, ld(own, k, col_b) + ld(rb1, k, pl.multiple_of(root * W, W)))
-
-        arrived(A1, k)
-
-        @pl.when(outer)
-        def _():
-            free(A2, k)
-            sa2[slot] = (ld(own, k, col_a) + ld(ra1, k)).astype(BF16)
-            message(A2, k).start()
-
-        @pl.when(inner)
-        def _():
-            st(own, k, col_a, ld(own, k, col_a) + ld(ra1, k))
-
-    def e3(k):
-        slot = lax.rem(k, NS)
-
-        @pl.when(inner)
+            send_sum(B2, sb2, k, mine_of(k, off_side, WA, WB) + half_of(rb1, k, off_side))
+            keep(k, side, WA, WB, mine_of(k, side, WA, WB) + half_of(rb1, k, side))
+
+    def b3(k):
+        @on_inner
         def _():
             arrived(B2, k)
-            free(B3, k)
-            sb3[slot] = (ld(own, k, col_b) + ld(rb2, k)).astype(BF16)
-            message(B3, k).start()
-            arrived(A2, k)
-            free(A3, k)
-            sa3[slot] = (ld(own, k, col_a) + ld(ra2, k)).astype(BF16)
-            message(A3, k).start()
-
-    def e4(k):
-        slot = lax.rem(k, NS)
-
-        @pl.when(inner)
+            send_sum(B3, sb3, k, mine_of(k, side, WA, WB) + got(rb2, k)[...].astype(F32))
+
+    def b4(k):
+        @on_inner
         def _():
             arrived(B3, k)
-            st(fin, k, pl.multiple_of(base + col_b, W), (sb3[slot].astype(F32) + ld(rb3, k)).astype(BF16))
-            free(FBI, k)
-            message(FBI, k).start()
-            free(FBO, k)
-            message(FBO, k).start()
-            arrived(A3, k)
-            st(fin, k, pl.multiple_of(base + col_a, W), (sa3[slot].astype(F32) + ld(ra3, k)).astype(BF16))
-            free(FAO, k)
-            message(FAO, k).start()
-            free(FAY, k)
-            message(FAY, k).start()
-
-    def e5(k):
-        @pl.when(inner)
+            put_final(k, side, WA, WB, sb3, got(rb3, k))
+            pass_on(FBI, k)
+            pass_on(FBO, k)
+
+    def b5(k):
+        @on_inner
         def _():
             arrived(FBI, k)
-            free(FB2, k)
-            message(FB2, k).start()
-
-        @pl.when(outer)
-        def _():
-            arrived(FAO, k)
-            free(FAY, k)
-            message(FAY, k).start()
-
-    def e6(k):
-        @pl.when(outer)
+            pass_on(FB2, k)
+            pass_on(FDB, k)
+
+    def b6(k):
+        @on_outer
         def _():
             arrived(FBO, k)
             arrived(FB2, k)
-
-        arrived(FAY, k)
-        free(FD, k)
-        message(FD, k).start()
-
-    def e7(k):
-        arrived(FD, k)
-
-    events = [(e1, 1), (e2, 1 + LAG), (e3, 1 + 2 * LAG), (e4, 1 + 3 * LAG), (e5, 1 + 4 * LAG), (e6, 1 + 5 * LAG), (e7, 2 + 5 * LAG)]
-    steps = S + 2 + 5 * LAG
+            pass_on(FDB, k)
+
+    def c1(k):
+        @on_outer
+        def _():
+            send_sum(C1, sb2, k, with_mate(k, off_side, WA, WB))
+            keep(k, side, WA, WB, with_mate(k, side, WA, WB))
+
+        @on_inner
+        def _():
+            keep(k, None, WA, WB, with_mate(k, None, WA, WB))
+
+    def c2(k):
+        @on_inner
+        def _():
+            arrived(C1, k)
+            send_sum(C2, sb2, k, mine_of(k, off_side, WA, WB) + pair(rb4, k)[...].astype(F32))
+
+    def c3(k):
+        @on_inner
+        def _():
+            arrived(C2, k)
+            send_sum(C3, sb3, k, mine_of(k, side, WA, WB) + got(rb2, k)[...].astype(F32))
+
+    def c4(k):
+        @on_outer
+        def _():
+            arrived(C3, k)
+            send_sum(C4, sb4, k, mine_of(k, side, WA, WB) + got(rb3, k)[...].astype(F32))
+
+    def c5(k):
+        @on_outer
+        def _():
+            arrived(C4, k)
+            put_final(k, side, WA, WB, sb4, pair(rb4, k))
+            pass_on(FC1, k)
+
+    def c6(k):
+        @on_inner
+        def _():
+            arrived(FC1, k)
+            pass_on(FC2, k)
+
+    def c7(k):
+        @on_inner
+        def _():
+            arrived(FC2, k)
+            pass_on(FC3, k)
+            pass_on(FDB, k)
+
+    def c8(k):
+        @on_outer
+        def _():
+            arrived(FC3, k)
+            pass_on(FDB, k)
+
+    events = (
+        [(event, 0, at) for event, at in zip((b1, b2, b3, b4, b5, b6), B_AT)]
+        + [(event, 1, at) for event, at in zip((c1, c2, c3, c4, c5, c6, c7, c8), C_AT)]
+        + [(event, None, at) for event, at in zip((a1, a2, a3, a4, a5, a6), A_AT)]
+    )
+    events.sort(key=lambda entry: (entry[2], entry[0] is a1 and -1))
+    steps = max(at for _, _, at in events) + S
 
     def step(s, _):
-        for event, offset in events:
-            @pl.when(jnp.logical_and(s >= offset, s < S + offset))
-            def _(event=event, offset=offset):
-                event(s - offset)
+        for event, parity, offset in events:
+            k = s - offset
+            due = jnp.logical_and(k >= 0, k < S)
+            if parity is not None:
+                due = jnp.logical_and(due, lax.rem(k + S, 2) == parity)
+
+            @pl.when(due)
+            def _(event=event, k=k):
+                event(k)
 
         @pl.when(jnp.logical_and(lax.rem(s, 2) == 0, s < 2 * NB))
         def _():
@@ -353,20 +450,32 @@
     for b in (NB - 2, NB - 1):
         term_copy(b).wait_send()
 
-    def drain(kinds):
+    def landed(k, _):
+        arrived(FDA, k)
+        arrived(FDB, k)
+        return 0
+
+    lax.fori_loop(0, S, landed, 0)
+
+    def drain(kinds, parity=None):
         for kind in kinds:
             for k in range(S - NS, S):
-                message(kind, k).wait_send()
-
-    drain((A1, FAY, FD))
-
-    @pl.when(inner)
+                if parity is None or k % 2 == parity:
+                    message(kind, k).wait_send()
+
+    drain((A1, FAY, FDA, FDB))
+
+    @on_inner
     def _():
-        drain((A3, B2, B3, FAO, FBO, FBI, FB2))
-
-    @pl.when(outer)
+        drain((A3, FAO))
+        drain((B2, B3, FBO, FBI, FB2), 0)
+        drain((C2, C3, FC2, FC3), 1)
+
+    @on_outer
     def _():
-        drain((A2, B1))
+        drain((A2,))
+        drain((B1,), 0)
+        drain((C1, C4, FC1), 1)
 
 
 PIECES = 4
@@ -392,16 +501,16 @@
         dma = pltpu.SemaphoreType.DMA
         scratch = [
             vmem((M, HALF), F32), vmem((M, HALF), BF16),
-            vmem((M, W), BF16), vmem((M, W), BF16), vmem((M, W), BF16),
-            vmem((M, 2 * W), BF16), vmem((M, W), BF16), vmem((M, W), BF16),
+            *[vmem((M // 2, WA), BF16)] * 3,
+            vmem((M // 2, WB), BF16), *[vmem((M // 2, WB), BF16)] * 2, vmem((M // 4, WB), BF16),
             vmem((2, TB, HALF), BF16),
-            vmem((NS, R, W), BF16), vmem((NS, R, W), BF16), vmem((NS, R, W), BF16),
-            vmem((NS, R, 2 * W), BF16), vmem((NS, R, W), BF16), vmem((NS, R, W), BF16),
+            *[vmem((NS, H, WA), BF16)] * 3,
+            vmem((NS, R, WB), BF16), *[vmem((NS, H, WB), BF16)] * 3,
             vmem((D, 2 * F), BF16), vmem((F, D), BF16),
             vmem((2, TB, D), BF16), vmem((2, TB, F), BF16), vmem((2, TB, F), BF16),
             vmem((M, 2 * F), BF16), vmem((F, M), BF16),
             vmem((2, M, TB), BF16), vmem((TB, M), BF16),
-            dma((KINDS, NS)), dma((KINDS, S)), dma((2,)), dma((NB,)), dma((3,)), dma((2, 3)), dma((2,)),
+            dma((ROWS, NS)), dma((ROWS, S)), dma((2,)), dma((NB,)), dma((3,)), dma((2, 3)), dma((2,)),
         ]
         anywhere = pl.BlockSpec(memory_space=pl.ANY)
         shape = jax.ShapeDtypeStruct

time: 106 us -> 103 us (0.972)
  Pallas kernels: 105 us -> 102 us
    pallas_call x1, Pallas kernels: 99.7 us -> 96.8 us  [step(): pl.pallas_call(kernel, out_shape=tuple((vmem(dims, BF16) for dims in shap...]
where the time goes in v3:
time: 103 us
  Pallas kernels  102 us (99%)
    pallas_call x1, Pallas kernels, step(): pl.pallas_call(kernel, out_shape=tuple((vmem(dims, BF16) for dims in shap...  96.8 us
    pallas_call x1, Pallas kernels, step(): pl.pallas_call(write_out, out_shape=tuple((shape(dims, BF16) for dims in...  5.31 us

profile of v3, /device:TPU:0, one launch (start us, length us, event | category | flops | bytes accessed | tf_op | source)
XLA Modules:
  0.0 102.7 jit_solution(10237275519051325961)
XLA Ops:
  0.6 96.8 %shard_map.102 = (bf16[2048,2048]{1,0:T(8,128)(2,1)S(1)}, bf16[2048,512]{1,0:T(8,128)(2,1)S(1)}, bf16[2048,512]{1,0:T(8,128)(2,1)S(1)}, bf16[512,2048]{1,0:T(8,128)(2,1)S(1)}) custom-call(bf16[2048,2048]{1,0:T(8,128)(2,1)} %x_hbm.1, bf16[2048,2048]{1,0:T(8,128)(2,1)} %dy_hbm.1, bf16[2048,512]{1,0:T(8,128)(2,1)} %gate_hbm.1, bf16[2048,512]{1,0:T(8,128)(2,1)} %up_hbm.1, ...), custom_call_target="tpu_custom_call" | custom-call | tf_op jit(solution)/shard_map/pallas_call | solution.py:518
  97.4 5.3 %shard_map.103 = (bf16[2048,2048]{1,0:T(8,128)(2,1)}, bf16[2048,512]{1,0:T(8,128)(2,1)}, bf16[2048,512]{1,0:T(8,128)(2,1)}, bf16[512,2048]{1,0:T(8,128)(2,1)}) custom-call(bf16[2048,2048]{1,0:T(8,128)(2,1)S(1)} %get-tuple-element.8.refs_0_, bf16[2048,512]{1,0:T(8,128)(2,1)S(1)} %get-tuple-element.9.refs_1_, bf16[2048,512]{1,0:T(8,128)(2,1)S(1)} %get-tuple-element.10.refs_2_, ...), custom_call_target="tpu_custom_call" | custom-call | tf_op jit(solution)/shard_map/pallas_call | solution.py:526

commit v4 on v3

--- a/solution.py
+++ b/solution.py
@@ -18,9 +18,9 @@
 S = M // R
 TB = 256
 NB = M // TB
-A_AT = (1, 5, 7, 9, 13, 18)
-B_AT = (3, 5, 7, 10, 12, 16)
-C_AT = (1, 3, 5, 8, 10, 12, 14, 18)
+A_AT = (3, 6, 8, 10, 15, 20)
+B_AT = (3, 5, 7, 10, 12, 18)
+C_AT = (3, 5, 7, 9, 11, 13, 15, 25)
 NS = 4
 LIMIT = 48 * 1024 * 1024
 
@@ -76,7 +76,7 @@
         ]
 
     def tile_copy(ref, i):
-        slot = lax.rem(i, 2)
+        slot = 0 if ref is x_hbm else 1
         return pltpu.make_async_copy(ref.at[:, pl.ds(i * TB, TB)], tile.at[slot], tilesem.at[slot])
 
     wcopies[0].start()
@@ -84,10 +84,6 @@
         copy.start()
     wcopies[1].start()
     wcopies[2].start()
-    for copy in block_copies(1):
-        copy.start()
-    tile_copy(x_hbm, 0).start()
-    tile_copy(x_hbm, 1).start()
 
     @pl.when(inner)
     def _():
@@ -103,7 +99,7 @@
             term_s.at[slot], term_r.at[rows, :], tsend.at[slot], trecv.at[b],
             device_id={"tp": mate}, device_id_type=MESH)
 
-    def terms(b):
+    def hidden_grads(b):
         slot = lax.rem(b, 2)
         row = pl.multiple_of(b * TB, TB)
         rows = pl.ds(row, TB)
@@ -125,10 +121,24 @@
             dgu[rows, F + n * 256:F + (n + 1) * 256] = (dh * silu).astype(BF16)
             hid_t[cols, rows] = (silu * u).T.astype(BF16)
 
+        @pl.when(b == 0)
+        def _():
+            for copy in block_copies(1):
+                copy.start()
+
         @pl.when(b + 2 < NB)
         def _():
             for copy in block_copies(b + 2):
                 copy.start()
+
+        @pl.when(b == NB - 1)
+        def _():
+            tile_copy(x_hbm, 0).start()
+            tile_copy(dy_hbm, 0).start()
+
+    def terms_other(b):
+        slot = lax.rem(b, 2)
+        rows = pl.ds(pl.multiple_of(b * TB, TB), TB)
 
         @pl.when(b == 0)
         def _():
@@ -143,41 +153,40 @@
             t = dot(dgu[rows, :], wgu[pl.ds(pl.multiple_of((1 - c) * HALF + n * 256, 256), 256), :], NT)
             term_s[slot, :, n * 256:(n + 1) * 256] = t.astype(BF16)
         term_copy(b).start()
+
+    def terms_own(b):
+        rows = pl.ds(pl.multiple_of(b * TB, TB), TB)
         for n in range(HALF // 256):
             t = dot(dgu[rows, :], wgu[pl.ds(pl.multiple_of(c * HALF + n * 256, 256), 256), :], NT)
             own[rows, n * 256:(n + 1) * 256] = t
 
-    def dw_gate_up(i):
-        slot = lax.rem(i, 2)
+    def dw_gate(i):
         tile_copy(x_hbm, i).wait()
         for j in range(M // 256):
-            tile_t[:, j * 256:(j + 1) * 256] = tile[slot, j * 256:(j + 1) * 256, :].T
-
-        @pl.when(i + 2 < NB)
-        def _():
-            tile_copy(x_hbm, i + 2).start()
-
-        @pl.when(i + 2 >= NB)
-        def _():
-            tile_copy(dy_hbm, i + 2 - NB).start()
+            tile_t[:, j * 256:(j + 1) * 256] = tile[0, j * 256:(j + 1) * 256, :].T
+
+        @pl.when(i + 1 < NB)
+        def _():
+            tile_copy(x_hbm, i + 1).start()
 
         rows = pl.ds(pl.multiple_of(i * TB, TB), TB)
         for n in range(F // 256):
-            cols = slice(n * 256, (n + 1) * 256)
-            dwg[rows, cols] = dot(tile_t[...], dgu[:, n * 256:(n + 1) * 256], NN).astype(BF16)
-            dwu[rows, cols] = dot(tile_t[...], dgu[:, F + n * 256:F + (n + 1) * 256], NN).astype(BF16)
+            dwg[rows, n * 256:(n + 1) * 256] = dot(tile_t[...], dgu[:, n * 256:(n + 1) * 256], NN).astype(BF16)
+
+    def dw_up(i):
+        rows = pl.ds(pl.multiple_of(i * TB, TB), TB)
+        for n in range(F // 256):
+            dwu[rows, n * 256:(n + 1) * 256] = dot(tile_t[...], dgu[:, F + n * 256:F + (n + 1) * 256], NN).astype(BF16)
 
     def dw_down(i):
-        slot = lax.rem(i, 2)
         tile_copy(dy_hbm, i).wait()
-
         cols = pl.ds(pl.multiple_of(i * TB, TB), TB)
         for n in range(F // 256):
-            dwd[n * 256:(n + 1) * 256, cols] = dot(hid_t[n * 256:(n + 1) * 256, :], tile[slot], NN).astype(BF16)
-
-        @pl.when(i + 2 < NB)
-        def _():
-            tile_copy(dy_hbm, i + 2).start()
+            dwd[n * 256:(n + 1) * 256, cols] = dot(hid_t[n * 256:(n + 1) * 256, :], tile[1], NN).astype(BF16)
+
+        @pl.when(i + 1 < NB)
+        def _():
+            tile_copy(dy_hbm, i + 1).start()
 
     base = pl.multiple_of(c * HALF, HALF)
     side, off_side = root, 1 - root
@@ -420,6 +429,9 @@
     events.sort(key=lambda entry: (entry[2], entry[0] is a1 and -1))
     steps = max(at for _, _, at in events) + S
 
+    term_units = hidden_grads, terms_other, terms_own
+    grad_units = dw_gate, dw_up, dw_down
+
     def step(s, _):
         for event, parity, offset in events:
             k = s - offset
@@ -431,17 +443,13 @@
             def _(event=event, k=k):
                 event(k)
 
-        @pl.when(jnp.logical_and(lax.rem(s, 2) == 0, s < 2 * NB))
-        def _():
-            terms(s // 2)
-
-        @pl.when(jnp.logical_and(s >= 2 * NB, s < 3 * NB))
-        def _():
-            dw_gate_up(s - 2 * NB)
-
-        @pl.when(jnp.logical_and(s >= 3 * NB, s < 4 * NB))
-        def _():
-            dw_down(s - 3 * NB)
+        for first, units in ((0, term_units), (len(term_units) * NB, grad_units)):
+            for i, unit in enumerate(units):
+                due = jnp.logical_and(s >= first, s < first + len(units) * NB)
+
+                @pl.when(jnp.logical_and(due, lax.rem(s, len(units)) == (first + i) % len(units)))
+                def _(unit=unit, first=first, n=len(units)):
+                    unit((s - first) // n)
 
         return 0
 

time: 103 us -> 100 us (0.971)
  Pallas kernels: 102 us -> 99.3 us
    pallas_call x1, Pallas kernels: 96.8 us -> 94 us  [step(): pl.pallas_call(kernel, out_shape=tuple((vmem(dims, BF16) for dims in shap...]
where the time goes in v4:
time: 100 us
  Pallas kernels  99.3 us (99%)
    pallas_call x1, Pallas kernels, step(): pl.pallas_call(kernel, out_shape=tuple((vmem(dims, BF16) for dims in shap...  94 us
    pallas_call x1, Pallas kernels, step(): pl.pallas_call(write_out, out_shape=tuple((shape(dims, BF16) for dims in...  5.31 us

profile of v4, /device:TPU:0, one launch (start us, length us, event | category | flops | bytes accessed | tf_op | source)
XLA Modules:
  0.0 100.0 jit_solution(17332001529781448893)
XLA Ops:
  0.6 94.0 %shard_map.102 = (bf16[2048,2048]{1,0:T(8,128)(2,1)S(1)}, bf16[2048,512]{1,0:T(8,128)(2,1)S(1)}, bf16[2048,512]{1,0:T(8,128)(2,1)S(1)}, bf16[512,2048]{1,0:T(8,128)(2,1)S(1)}) custom-call(bf16[2048,2048]{1,0:T(8,128)(2,1)} %x_hbm.1, bf16[2048,2048]{1,0:T(8,128)(2,1)} %dy_hbm.1, bf16[2048,512]{1,0:T(8,128)(2,1)} %gate_hbm.1, bf16[2048,512]{1,0:T(8,128)(2,1)} %up_hbm.1, ...), custom_call_target="tpu_custom_call" | custom-call | tf_op jit(solution)/shard_map/pallas_call | solution.py:526
  94.6 5.3 %shard_map.103 = (bf16[2048,2048]{1,0:T(8,128)(2,1)}, bf16[2048,512]{1,0:T(8,128)(2,1)}, bf16[2048,512]{1,0:T(8,128)(2,1)}, bf16[512,2048]{1,0:T(8,128)(2,1)}) custom-call(bf16[2048,2048]{1,0:T(8,128)(2,1)S(1)} %get-tuple-element.8.refs_0_, bf16[2048,512]{1,0:T(8,128)(2,1)S(1)} %get-tuple-element.9.refs_1_, bf16[2048,512]{1,0:T(8,128)(2,1)S(1)} %get-tuple-element.10.refs_2_, ...), custom_call_target="tpu_custom_call" | custom-call | tf_op jit(solution)/shard_map/pallas_call | solution.py:534

commit v5 on v4

--- a/solution.py
+++ b/solution.py
@@ -18,9 +18,9 @@
 S = M // R
 TB = 256
 NB = M // TB
-A_AT = (3, 6, 8, 10, 15, 20)
-B_AT = (3, 5, 7, 10, 12, 18)
-C_AT = (3, 5, 7, 9, 11, 13, 15, 25)
+A_AT = (3, 6, 8, 10, 14, 17)
+B_AT = (3, 5, 7, 10, 12, 19)
+C_AT = (3, 5, 7, 9, 11, 13, 15, 21)
 NS = 4
 LIMIT = 48 * 1024 * 1024
 
@@ -422,11 +422,12 @@
             pass_on(FDB, k)
 
     events = (
-        [(event, 0, at) for event, at in zip((b1, b2, b3, b4, b5, b6), B_AT)]
-        + [(event, 1, at) for event, at in zip((c1, c2, c3, c4, c5, c6, c7, c8), C_AT)]
+        [(event, 1, at) for event, at in zip((b1, b2, b3, b4, b5, b6), B_AT)]
+        + [(event, 0, at) for event, at in zip((c1, c2, c3, c4, c5, c6, c7, c8), C_AT)]
         + [(event, None, at) for event, at in zip((a1, a2, a3, a4, a5, a6), A_AT)]
     )
-    events.sort(key=lambda entry: (entry[2], entry[0] is a1 and -1))
+    order = (c2, c3, a1, c8, b3, b1, c4, b2, c1, a2, b6, a3, a4, c5, a6, b4, c6, a5, b5, c7)
+    events.sort(key=lambda entry: order.index(entry[0]))
     steps = max(at for _, _, at in events) + S
 
     term_units = hidden_grads, terms_other, terms_own
@@ -476,14 +477,14 @@
     @on_inner
     def _():
         drain((A3, FAO))
-        drain((B2, B3, FBO, FBI, FB2), 0)
-        drain((C2, C3, FC2, FC3), 1)
+        drain((B2, B3, FBO, FBI, FB2), 1)
+        drain((C2, C3, FC2, FC3), 0)
 
     @on_outer
     def _():
         drain((A2,))
-        drain((B1,), 0)
-        drain((C1, C4, FC1), 1)
+        drain((B1,), 1)
+        drain((C1, C4, FC1), 0)
 
 
 PIECES = 4

time: 100 us -> 98.3 us (0.983)
  Pallas kernels: 99.3 us -> 97.5 us
    pallas_call x1, Pallas kernels: 94 us -> 92.2 us  [step(): pl.pallas_call(kernel, out_shape=tuple((vmem(dims, BF16) for dims in shap...]
where the time goes in v5:
time: 98.3 us; the launch traced here: 98.2 us
  Pallas kernels  97.5 us (99%)
    pallas_call x1, Pallas kernels, step(): pl.pallas_call(kernel, out_shape=tuple((vmem(dims, BF16) for dims in shap...  92.2 us
    pallas_call x1, Pallas kernels, step(): pl.pallas_call(write_out, out_shape=tuple((shape(dims, BF16) for dims in...  5.31 us

profile of v5, /device:TPU:0, one launch (start us, length us, event | category | flops | bytes accessed | tf_op | source)
XLA Modules:
  0.0 98.2 jit_solution(13578557298945541453)
XLA Ops:
  0.6 92.2 %shard_map.102 = (bf16[2048,2048]{1,0:T(8,128)(2,1)S(1)}, bf16[2048,512]{1,0:T(8,128)(2,1)S(1)}, bf16[2048,512]{1,0:T(8,128)(2,1)S(1)}, bf16[512,2048]{1,0:T(8,128)(2,1)S(1)}) custom-call(bf16[2048,2048]{1,0:T(8,128)(2,1)} %x_hbm.1, bf16[2048,2048]{1,0:T(8,128)(2,1)} %dy_hbm.1, bf16[2048,512]{1,0:T(8,128)(2,1)} %gate_hbm.1, bf16[2048,512]{1,0:T(8,128)(2,1)} %up_hbm.1, ...), custom_call_target="tpu_custom_call" | custom-call | tf_op jit(solution)/shard_map/pallas_call | solution.py:527
  92.9 5.3 %shard_map.103 = (bf16[2048,2048]{1,0:T(8,128)(2,1)}, bf16[2048,512]{1,0:T(8,128)(2,1)}, bf16[2048,512]{1,0:T(8,128)(2,1)}, bf16[512,2048]{1,0:T(8,128)(2,1)}) custom-call(bf16[2048,2048]{1,0:T(8,128)(2,1)S(1)} %get-tuple-element.8.refs_0_, bf16[2048,512]{1,0:T(8,128)(2,1)S(1)} %get-tuple-element.9.refs_1_, bf16[2048,512]{1,0:T(8,128)(2,1)S(1)} %get-tuple-element.10.refs_2_, ...), custom_call_target="tpu_custom_call" | custom-call | tf_op jit(solution)/shard_map/pallas_call | solution.py:535

commit v6 on v5

--- a/solution.py
+++ b/solution.py
@@ -426,7 +426,7 @@
         + [(event, 0, at) for event, at in zip((c1, c2, c3, c4, c5, c6, c7, c8), C_AT)]
         + [(event, None, at) for event, at in zip((a1, a2, a3, a4, a5, a6), A_AT)]
     )
-    order = (c2, c3, a1, c8, b3, b1, c4, b2, c1, a2, b6, a3, a4, c5, a6, b4, c6, a5, b5, c7)
+    order = (a1, c2, c3, b2, b3, c4, c1, b1, a2, a3, c5, a4, b4, c6, a5, b5, c7, c8, b6, a6)
     events.sort(key=lambda entry: order.index(entry[0]))
     steps = max(at for _, _, at in events) + S
 
@@ -487,7 +487,7 @@
         drain((C1, C4, FC1), 0)
 
 
-PIECES = 4
+PIECES = 2
 
 
 def write_out(*refs):

time: 98.3 us -> 98.1 us (level)
  no operation moved by 1% of the time
where the time goes in v6:
time: 98.1 us; the launch traced here: 97.9 us
  Pallas kernels  97.3 us (99%)
    pallas_call x1, Pallas kernels, step(): pl.pallas_call(kernel, out_shape=tuple((vmem(dims, BF16) for dims in shap...  92 us
    pallas_call x1, Pallas kernels, step(): pl.pallas_call(write_out, out_shape=tuple((shape(dims, BF16) for dims in...  5.26 us

profile of v6, /device:TPU:0, one launch (start us, length us, event | category | flops | bytes accessed | tf_op | source)
XLA Modules:
  0.0 97.9 jit_solution(3319529459481161018)
XLA Ops:
  0.6 92.0 %shard_map.102 = (bf16[2048,2048]{1,0:T(8,128)(2,1)S(1)}, bf16[2048,512]{1,0:T(8,128)(2,1)S(1)}, bf16[2048,512]{1,0:T(8,128)(2,1)S(1)}, bf16[512,2048]{1,0:T(8,128)(2,1)S(1)}) custom-call(bf16[2048,2048]{1,0:T(8,128)(2,1)} %x_hbm.1, bf16[2048,2048]{1,0:T(8,128)(2,1)} %dy_hbm.1, bf16[2048,512]{1,0:T(8,128)(2,1)} %gate_hbm.1, bf16[2048,512]{1,0:T(8,128)(2,1)} %up_hbm.1, ...), custom_call_target="tpu_custom_call" | custom-call | tf_op jit(solution)/shard_map/pallas_call | solution.py:527
  92.7 5.3 %shard_map.103 = (bf16[2048,2048]{1,0:T(8,128)(2,1)}, bf16[2048,512]{1,0:T(8,128)(2,1)}, bf16[2048,512]{1,0:T(8,128)(2,1)}, bf16[512,2048]{1,0:T(8,128)(2,1)}) custom-call(bf16[2048,2048]{1,0:T(8,128)(2,1)S(1)} %get-tuple-element.8.refs_0_, bf16[2048,512]{1,0:T(8,128)(2,1)S(1)} %get-tuple-element.9.refs_1_, bf16[2048,512]{1,0:T(8,128)(2,1)S(1)} %get-tuple-element.10.refs_2_, ...), custom_call_target="tpu_custom_call" | custom-call | tf_op jit(solution)/shard_map/pallas_call | solution.py:535
